TPU v7x, 256 devices: a 4x2x16 block of a 4x16x16 slice. The times are simulated.
256 devices in a mesh: groups: 2 (over y), mp: 16 (over z), expert: 4 (over x), dp: 2 (over core).
Axes of the slice: x: 4, y: 2, z: 16, core: 2. Of those that a mesh axis runs over, the one named last changes fastest.
The devices are a block of a 4x16x16 slice.
Arguments:
- hidden_in: bfloat16 [1024, 4096], P(('groups', 'expert', 'dp'), 'mp'), parts along dimension 0, may hold values from -6 to 6
- norm_gain: bfloat16 [2, 4096], P(None, 'mp'), may hold values from 0.25 to 1.75
- expert_ids: int32 [2, 1024, 2], P(None, ('groups', 'expert', 'dp')), parts along dimension 1, may hold values from 0 to 3, all different within a row; in each aligned block of 64 rows (0 to 63, 64 to 127, ..., all dimensions but the last counted through in order) at most 64 rows name the same one
- gate_counts: int32 [2, 1024, 2], P(None, ('groups', 'expert', 'dp')), parts along dimension 1, may hold values from 8 to 15
- exit_layer: int32 [1024], P(('groups', 'expert', 'dp')), parts along dimension 0, may hold values from 1 to 2
- w_gate: bfloat16 [2, 4, 7168, 4096], P(None, 'expert', ('mp', 'dp')), may hold values from -0.09375 to 0.09375
- w_up: bfloat16 [2, 4, 7168, 4096], P(None, 'expert', ('mp', 'dp')), may hold values from -0.09375 to 0.09375
- w_down: bfloat16 [2, 4, 7168, 4096], P(None, 'expert', ('mp', 'dp')), may hold values from -0.0625 to 0.0625
Outputs:
- hidden_out: bfloat16 [1024, 4096], P(('groups', 'expert', 'dp'), 'mp'), parts along dimension 0
There are 2 independent parts, one for each index of `groups`. A program takes and returns all parts, laid end to end along the dimension named above; an argument that names none is the same for every part. Nothing has to cross between parts.
Inputs may be any that keep to these rules, and one draw needn't show every extreme that they name: `expert_ids`: A token's two ids in a layer differ. In the rows of one device in one layer (aligned blocks of 64 rows, layer by layer) some expert may be named by all 64 rows.
All inputs are finite; a program needn't handle non-finite values.
Results may differ from a plain program's by a relative error of at most 0.014.
Values may be sent and summed in bfloat16 or wider, within the bound.
A program may use at most 128 MiB of HBM per device.

v0:
```python
import jax
import jax.numpy as jnp
from jax import lax
from jax.sharding import PartitionSpec as P

LAYERS = 2
norm_floor = 0.1


def rows_first(arrays, axis, dims):
    turned = [jnp.moveaxis(a, dim, 0) for a, dim in zip(arrays, dims)]
    both = jnp.concatenate([t.reshape(len(t), -1) for t in turned], axis=1)
    whole, at, outs = (lax.all_gather(both, axis, axis=0, tiled=True), 0, [])
    for t, dim in zip(turned, dims):
        section = whole[:, at : at + t[0].size].reshape(-1, *t.shape[1:])
        outs.append(jnp.moveaxis(section, 0, dim))
        at += t[0].size
    return tuple(outs)


def side_by_side(arrays, axis, dim, along):
    ends, at = ([], 0)
    for a in arrays[:-1]:
        at += a.shape[along]
        ends.append(at)
    both = jnp.concatenate(arrays, axis=along)
    return tuple(jnp.split(lax.all_gather(both, axis, axis=dim, tiled=True), ends, axis=along))


def body(hidden_in, norm_gain, expert_ids, gate_counts, exit_layer, w_gate, w_up, w_down):
    experts = lax.axis_size("expert")
    shards = lax.axis_size("mp")
    tok_rows, slice_width = hidden_in.shape
    full_width = slice_width * shards
    contract = (((1,), (1,)), ((), ()))
    expert_range = jnp.arange(experts, dtype=jnp.int32)
    slot_range = jnp.arange(tok_rows, dtype=jnp.int32)
    current = hidden_in
    for layer_idx in range(LAYERS):
        counts = gate_counts[layer_idx].astype(jnp.float32)
        gate_share = counts / jnp.sum(counts, axis=1, keepdims=True)
        active = exit_layer > layer_idx
        matched = (expert_ids[layer_idx][:, :, None] == expert_range[None, None, :]) & active[
            :, None, None
        ]
        chosen = jnp.sum(matched.astype(jnp.int32), axis=1)
        weight_te = jnp.sum(jnp.where(matched, gate_share[:, :, None], jnp.float32(0.0)), axis=1)
        slot_rank = jnp.cumsum(chosen, axis=0) - chosen
        place_mask = (slot_rank.T[:, None, :] == slot_range[None, :, None]) & (
            chosen.T[:, None, :] > 0
        )
        place_bf = place_mask.astype(jnp.bfloat16)
        current_f32 = current.astype(jnp.float32)
        whole_rows, whole_gain = rows_first((current, norm_gain[layer_idx]), "mp", (1, 0))
        whole_f32 = whole_rows.astype(jnp.float32)
        sum_squares = jnp.sum(whole_f32 * whole_f32, axis=1)
        inv_rms = lax.rsqrt(sum_squares / full_width + norm_floor)
        normed = (whole_f32 * inv_rms[:, None] * whole_gain.astype(jnp.float32)[None, :]).astype(
            jnp.bfloat16
        )
        outgoing = jnp.einsum(
            "ect,td->ecd", place_bf, normed, preferred_element_type=jnp.float32
        ).astype(jnp.bfloat16)
        incoming = lax.all_to_all(outgoing, "expert", split_axis=0, concat_axis=0, tiled=True)
        inputs = incoming.reshape(experts * tok_rows, full_width)
        gate_rows, up_rows, down_rows = side_by_side(
            (w_gate[layer_idx, 0], w_up[layer_idx, 0], w_down[layer_idx, 0]), "dp", 0, 1
        )
        gate_val = lax.dot_general(inputs, gate_rows, contract, preferred_element_type=jnp.float32)
        up_val = lax.dot_general(inputs, up_rows, contract, preferred_element_type=jnp.float32)
        hidden = (jax.nn.silu(gate_val) * up_val).astype(jnp.bfloat16)
        partial_value = jnp.dot(hidden, down_rows, preferred_element_type=jnp.float32)
        summed = lax.psum_scatter(
            partial_value.astype(jnp.bfloat16), "mp", scatter_dimension=1, tiled=True
        )
        returned = lax.all_to_all(
            summed.reshape(experts, tok_rows, slice_width),
            "expert",
            split_axis=0,
            concat_axis=0,
            tiled=True,
        )
        place_weight = place_mask.astype(jnp.float32) * weight_te.T[:, None, :]
        update = jnp.einsum("ect,ecd->td", place_weight, returned.astype(jnp.float32))
        current = (current_f32 + update).astype(jnp.bfloat16)
    return current


def solution(mesh):
    in_specs = (
        P(("groups", "expert", "dp"), "mp"),
        P(None, "mp"),
        P(None, ("groups", "expert", "dp"), None),
        P(None, ("groups", "expert", "dp"), None),
        P(("groups", "expert", "dp")),
        P(None, "expert", ("mp", "dp"), None),
        P(None, "expert", ("mp", "dp"), None),
        P(None, "expert", ("mp", "dp"), None),
    )
    out_specs = P(("groups", "expert", "dp"), "mp")
    return jax.shard_map(body, mesh=mesh, in_specs=in_specs, out_specs=out_specs, check_vma=False)
```

profile of v0, /device:TPU:40, one launch (start us, length us, event | category | flops | bytes accessed | tf_op | source)
XLA Modules:
  0.0 336.3 jit_solution(16841984590572916138)
XLA Ops:
  6.5 0.0 all-gather.3.cloned.1.call-start
  6.6 0.0 copy-start
  6.6 2.5 slice_bitcast_fusion.5
  9.1 0.6 copy-done
  9.7 1.1 copy-done.1
  10.8 2.8 slice_bitcast_fusion.3
  13.6 5.6 %pad_maximum_fusion = bf16[224,12288]{1,0:T(8,128)(2,1)} fusion(bf16[224,4096]{1,0:T(8,128)(2,1)S(1)} %get-tuple-element.11, bf16[224,4096]{1,0:T(8,128)(2,1)S(1)} %get-tuple-element.22, bf16[224,4096]{1,0:T(8,128)(2,1)S(1)} %get-tuple-element.7), kind=kLoop, calls=%fused_computation | loop fusion | flops 16515072 | bytes 11010048 | tf_op jit(solution)/shard_map/concatenate | solution.py:26
  19.1 0.1 all-gather.3.cloned.1.call-update
  19.2 0.1 reduce-scatter.3.cloned.1.call-start
  19.3 0.5 copy-done.6
  19.8 0.0 copy-done.5
  19.8 0.1 copy.19
  19.9 0.1 reduce_window_sum.17
  20.0 0.1 copy.21
  20.1 0.0 copy-done.4
  20.1 0.0 copy-done.2
  20.2 51.8 %all_gather.12 = bf16[4096,65]{0,1:T(8,128)(2,1)S(1)} all-gather(bf16[256,65]{0,1:T(8,128)(2,1)S(1)} %pad_maximum_fusion.2), channel_id=1, replica_groups=mesh['groups'=2,'mp'=16,'expert'=4,'dp'=2] {'mp'}, dimensions={0}, use_global_device_ids=true | all-gather | bytes 565760 | tf_op jit(solution)/shard_map/all_gather | solution.py:13
  72.0 0.2 fusion.30
  72.2 0.9 convolution_convert_fusion.3
  73.1 23.9 %all_to_all.20 = bf16[4,64,4096]{2,1,0:T(8,128)(2,1)} all-to-all(bf16[4,64,4096]{2,1,0:T(8,128)(2,1)S(1)} %convolution_convert_fusion.3), channel_id=1, replica_groups=mesh['groups'=2,'mp'=16,'expert'=4,'dp'=2] {'expert'}, dimensions={0} | all-to-all | bytes 4194304 | tf_op jit(solution)/shard_map/all_to_all | solution.py:64
  97.0 3.8 %fusion.8 = f32[256,448]{0,1:T(8,128)S(1)} fusion(bf16[256,4096]{1,0:T(8,128)(2,1)} %bitcast.68, bf16[448,12288]{1,0:T(8,128)(2,1)} %all-gather.3.cloned.1.call-done), kind=kOutput, calls=%fused_computation.14 | convolution fusion | flops 939524096 | bytes 6225920 | tf_op jit(solution)/shard_map/dot_general | solution.py:69
  100.8 9.4 %convolution_convert_fusion.2 = bf16[256,4096]{1,0:T(8,128)(2,1)} fusion(bf16[448,12288]{1,0:T(8,128)(2,1)} %all-gather.3.cloned.1.call-done, bf16[256,4096]{1,0:T(8,128)(2,1)} %bitcast.69, f32[256,448]{0,1:T(8,128)S(1)} %fusion.8), kind=kOutput, calls=%fused_computation.4 | convolution fusion | flops 1880784896 | bytes 11993088 | tf_op jit(solution)/shard_map/dot_general | solution.py:72
  110.2 0.1 reduce-scatter.3.cloned.1.call-update
  110.2 0.1 all-gather.5.cloned.1.call-start
  110.3 4.9 %pad_maximum_fusion.1 = bf16[224,12288]{1,0:T(8,128)(2,1)} fusion(bf16[224,4096]{1,0:T(8,128)(2,1)} %get-tuple-element.12, bf16[224,4096]{1,0:T(8,128)(2,1)} %get-tuple-element.21, bf16[224,4096]{1,0:T(8,128)(2,1)S(1)} %get-tuple-element.8), kind=kLoop, calls=%fused_computation.1 | loop fusion | flops 16515072 | bytes 11010048 | tf_op jit(solution)/shard_map/concatenate | solution.py:26
  115.2 0.1 all-gather.5.cloned.1.call-update
  115.3 0.1 copy.23
  115.4 0.1 reduce_window_sum.18
  115.5 0.1 copy.25
  115.6 0.3 copy-done.3
  115.9 57.0 %reduce-scatter.3.cloned.1.call-done = bf16[256,256]{1,0:T(8,128)(2,1)} async-done(((bf16[256,4096]{1,0:T(8,128)(2,1)}), bf16[256,256]{1,0:T(8,128)(2,1)}) %reduce-scatter.3.cloned.1.call-update) | async-done | bytes 131088 | tf_op jit(solution)/shard_map/reduce_scatter | solution.py:73
  172.9 4.3 %all-to-all-start.1 = ((bf16[4,64,256]{2,1,0:T(8,128)(2,1)}), bf16[4,64,256]{2,1,0:T(8,128)(2,1)S(1)}, u32[]{:S(2)}, u32[]{:S(2)}) async-start(bf16[4,64,256]{2,1,0:T(8,128)(2,1)} %bitcast.70), calls=%async_computation.2 | async-start | bytes 262144 | tf_op jit(solution)/shard_map/all_to_all | solution.py:76
  177.3 6.0 %all-to-all-done.1 = bf16[4,64,256]{2,1,0:T(8,128)(2,1)S(1)} async-done(((bf16[4,64,256]{2,1,0:T(8,128)(2,1)}), bf16[4,64,256]{2,1,0:T(8,128)(2,1)S(1)}, u32[]{:S(2)}, u32[]{:S(2)}) %all-to-all-start.1) | async-done | bytes 131104 | tf_op jit(solution)/shard_map/all_to_all | solution.py:76
  183.2 0.3 fusion.29
  183.5 30.7 %all_gather.14 = bf16[4096,65]{0,1:T(8,128)(2,1)S(1)} all-gather(bf16[256,65]{0,1:T(8,128)(2,1)S(1)} %pad_maximum_fusion.3), channel_id=1, replica_groups=mesh['groups'=2,'mp'=16,'expert'=4,'dp'=2] {'mp'}, dimensions={0}, use_global_device_ids=true | all-gather | bytes 565760 | tf_op jit(solution)/shard_map/all_gather | solution.py:13
  214.3 0.2 fusion.33
  214.5 2.2 convolution_convert_fusion.1
  216.7 3.7 %all-to-all-start.2 = ((bf16[4,64,4096]{2,1,0:T(8,128)(2,1)}), bf16[4,64,4096]{2,1,0:T(8,128)(2,1)S(1)}, u32[]{:S(2)}, u32[]{:S(2)}) async-start(bf16[4,64,4096]{2,1,0:T(8,128)(2,1)} %convolution_convert_fusion.1), calls=%async_computation.3 | async-start | bytes 4194304 | tf_op jit(solution)/shard_map/all_to_all | solution.py:64
  220.4 0.2 reduce-scatter.5.cloned.1.call-start
  220.7 0.0 all-gather.5.cloned.1.call-done
  220.7 16.1 %all-to-all-done.2 = bf16[4,64,4096]{2,1,0:T(8,128)(2,1)S(1)} async-done(((bf16[4,64,4096]{2,1,0:T(8,128)(2,1)}), bf16[4,64,4096]{2,1,0:T(8,128)(2,1)S(1)}, u32[]{:S(2)}, u32[]{:S(2)}) %all-to-all-start.2) | async-done | bytes 2097184 | tf_op jit(solution)/shard_map/all_to_all | solution.py:64
  236.8 3.2 fusion.3
  240.0 8.8 %convolution_convert_fusion = bf16[256,4096]{1,0:T(8,128)(2,1)} fusion(bf16[448,12288]{1,0:T(8,128)(2,1)} %all-gather.5.cloned.1.call-done, bf16[256,4096]{1,0:T(8,128)(2,1)S(1)} %bitcast.67, f32[256,448]{0,1:T(8,128)S(1)} %fusion.3), kind=kOutput, calls=%fused_computation.2 | convolution fusion | flops 1880784896 | bytes 11993088 | tf_op jit(solution)/shard_map/dot_general | solution.py:72
  248.8 0.1 reduce-scatter.5.cloned.1.call-update
  248.9 69.8 %reduce-scatter.5.cloned.1.call-done = bf16[256,256]{1,0:T(8,128)(2,1)} async-done(((bf16[256,4096]{1,0:T(8,128)(2,1)}), bf16[256,256]{1,0:T(8,128)(2,1)}) %reduce-scatter.5.cloned.1.call-update) | async-done | bytes 131088 | tf_op jit(solution)/shard_map/reduce_scatter | solution.py:73
  318.7 4.2 %all-to-all-start.3 = ((bf16[4,64,256]{2,1,0:T(8,128)(2,1)}), bf16[4,64,256]{2,1,0:T(8,128)(2,1)S(1)}, u32[]{:S(2)}, u32[]{:S(2)}) async-start(bf16[4,64,256]{2,1,0:T(8,128)(2,1)} %bitcast.71), calls=%async_computation.5 | async-start | bytes 262144 | tf_op jit(solution)/shard_map/all_to_all | solution.py:76
  322.9 6.0 %all-to-all-done.3 = bf16[4,64,256]{2,1,0:T(8,128)(2,1)S(1)} async-done(((bf16[4,64,256]{2,1,0:T(8,128)(2,1)}), bf16[4,64,256]{2,1,0:T(8,128)(2,1)S(1)}, u32[]{:S(2)}, u32[]{:S(2)}) %all-to-all-start.3) | async-done | bytes 131104 | tf_op jit(solution)/shard_map/all_to_all | solution.py:76
  328.9 0.9 fusion.28
  (26 shorter events, 0.2 us)
Async XLA Ops:
  6.5 90.4 %all-gather.3.cloned.1.call-start = ((), (), s32[]{:S(2)}) async-start(), calls=%async_computation.6 | async-start | bytes 16515072 | tf_op jit(solution)/shard_map/all_gather | solution.py:27
  6.6 3.1 copy-start
  6.6 4.3 %copy-start.1 = (bf16[2,1,224,4096]{3,2,1,0:T(8,128)(2,1)S(1)}, bf16[2,1,224,4096]{3,2,1,0:T(8,128)(2,1)}, u32[]{:S(2)}) copy-start(bf16[2,1,224,4096]{3,2,1,0:T(8,128)(2,1)} %param.14) | copy-start | bytes 11010052
  19.1 0.7 copy-start.6
  19.1 0.7 copy-start.5
  19.1 1.0 copy-start.4
  19.1 1.0 copy-start.2
  19.2 153.7 %reduce-scatter.3.cloned.1.call-start = ((), (), s32[]{:S(2)}) async-start(), calls=%async_computation.7 | async-start | bytes 2228224 | tf_op jit(solution)/shard_map/reduce_scatter | solution.py:73
  110.2 110.5 %all-gather.5.cloned.1.call-start = ((), (), s32[]{:S(2)}) async-start(), calls=%async_computation.8 | async-start | bytes 16515072 | tf_op jit(solution)/shard_map/all_gather | solution.py:27
  115.2 0.7 copy-start.3
  172.9 10.3 %all-to-all-start.1 = ((bf16[4,64,256]{2,1,0:T(8,128)(2,1)}), bf16[4,64,256]{2,1,0:T(8,128)(2,1)S(1)}, u32[]{:S(2)}, u32[]{:S(2)}) async-start(bf16[4,64,256]{2,1,0:T(8,128)(2,1)} %bitcast.70), calls=%async_computation.2 | async-start | bytes 262144 | tf_op jit(solution)/shard_map/all_to_all | solution.py:76
  216.7 20.1 %all-to-all-start.2 = ((bf16[4,64,4096]{2,1,0:T(8,128)(2,1)}), bf16[4,64,4096]{2,1,0:T(8,128)(2,1)S(1)}, u32[]{:S(2)}, u32[]{:S(2)}) async-start(bf16[4,64,4096]{2,1,0:T(8,128)(2,1)} %convolution_convert_fusion.1), calls=%async_computation.3 | async-start | bytes 4194304 | tf_op jit(solution)/shard_map/all_to_all | solution.py:64
  220.4 98.3 %reduce-scatter.5.cloned.1.call-start = ((), (), s32[]{:S(2)}) async-start(), calls=%async_computation.9 | async-start | bytes 2228224 | tf_op jit(solution)/shard_map/reduce_scatter | solution.py:73
  318.7 10.2 %all-to-all-start.3 = ((bf16[4,64,256]{2,1,0:T(8,128)(2,1)}), bf16[4,64,256]{2,1,0:T(8,128)(2,1)S(1)}, u32[]{:S(2)}, u32[]{:S(2)}) async-start(bf16[4,64,256]{2,1,0:T(8,128)(2,1)} %bitcast.71), calls=%async_computation.5 | async-start | bytes 262144 | tf_op jit(solution)/shard_map/all_to_all | solution.py:76
Sparse Core Ops, SparseCore 0:
  19.3 45.2 all-gather.2
  110.4 62.5 reduce-scatter.2
  174.8 29.9 all-gather.4
  249.0 69.6 reduce-scatter.4
where the time goes:
time: 337 us; the launch traced here: 336 us
  waiting for transfers between devices  155 us (46%)
  blocking collectives  106 us (31%)
  matrix products  29.4 us (9%)
  between operations  13.3 us (4%)
  starting transfers between devices  12.6 us (4%)
  other arithmetic  11.3 us (3%)
  local copies, waits for them, and re-layouts  8.24 us (2%)
    reduce_scatter x2, waiting for transfers between devices, body(): lax.psum_scatter(partial_value.astype(jnp.bfloat16), 'mp', scatter_dimens...  127 us
    all_gather x2, blocking collectives, rows_first(): whole, at, outs = (lax.all_gather(both, axis, axis=0, tiled=True), 0, [])  82.5 us
    all_to_all x1, blocking collectives, body(): lax.all_to_all(outgoing, 'expert', split_axis=0, concat_axis=0, tiled=True)  23.9 us
    dot_general x2, matrix products, body(): jnp.dot(hidden, down_rows, preferred_element_type=jnp.float32)  18.2 us
    all_to_all x1, waiting for transfers between devices, body(): lax.all_to_all(outgoing, 'expert', split_axis=0, concat_axis=0, tiled=True)  16.1 us
    all_to_all x2, waiting for transfers between devices, body(): lax.all_to_all(summed.reshape(experts, tok_rows, slice_width), 'expert',...  11.9 us
    concatenate x2, other arithmetic, side_by_side(): both = jnp.concatenate(arrays, axis=along)  10.5 us
    all_to_all x2, starting transfers between devices, body(): lax.all_to_all(summed.reshape(experts, tok_rows, slice_width), 'expert',...  8.52 us
  transfers between devices with their start and end apart: 7, of which 5 were waited for; matrix products, arithmetic and copies ran while one was open for 3% of the time, Pallas kernels for 0%

commit v1 on v0

--- a/solution.py
+++ b/solution.py
@@ -5,6 +5,18 @@
 
 LAYERS = 2
 norm_floor = 0.1
+
+
+def split_up(shard, dim, count):
+    lengths = shard.shape
+    blocks = shard.reshape(*lengths[:dim], count, lengths[dim] // count, *lengths[dim + 1 :])
+    return jnp.moveaxis(blocks, dim, 0)
+
+
+def in_order(parts, dim):
+    shape = list(parts.shape[1:])
+    shape[dim] *= parts.shape[0]
+    return jnp.moveaxis(parts, 0, dim).reshape(shape)
 
 
 def rows_first(arrays, axis, dims):
@@ -61,7 +73,15 @@
         outgoing = jnp.einsum(
             "ect,td->ecd", place_bf, normed, preferred_element_type=jnp.float32
         ).astype(jnp.bfloat16)
-        incoming = lax.all_to_all(outgoing, "expert", split_axis=0, concat_axis=0, tiled=True)
+        length, here = (lax.axis_size("expert"), lax.axis_index("expert"))
+        tiles = split_up(outgoing, 0, length)
+        out = tiles
+        for turn in range(1, length):
+            target, source = ((here + turn) % length, (here - turn) % length)
+            sent = lax.dynamic_index_in_dim(tiles, target, 0)
+            theirs = lax.ppermute(sent, "expert", [(i, (i + turn) % length) for i in range(length)])
+            out = lax.dynamic_update_slice_in_dim(out, theirs, source, axis=0)
+        incoming = in_order(out, 0)
         inputs = incoming.reshape(experts * tok_rows, full_width)
         gate_rows, up_rows, down_rows = side_by_side(
             (w_gate[layer_idx, 0], w_up[layer_idx, 0], w_down[layer_idx, 0]), "dp", 0, 1

time: 337 us -> 342 us (1.015)
  blocking collectives: 106 us -> 82.5 us
  waiting for transfers between devices: 155 us -> 166 us
  local copies, waits for them, and re-layouts: 8.24 us -> 19.2 us
  starting transfers between devices: 12.6 us -> 18.4 us
    ppermute x0 -> x6, waiting for transfers between devices: none -> 25.4 us  [body(): lax.ppermute(sent, 'expert', [(i, (i + turn) % length) for i in range(len...]
    all_to_all x1 -> x0, blocking collectives: 23.9 us -> none  [body(): lax.all_to_all(outgoing, 'expert', split_axis=0, concat_axis=0, tiled=True)]
    all_to_all x1 -> x0, waiting for transfers between devices: 16.1 us -> none  [body(): lax.all_to_all(outgoing, 'expert', split_axis=0, concat_axis=0, tiled=True)]
    ppermute x0 -> x6, starting transfers between devices: none -> 9.6 us  [body(): lax.ppermute(sent, 'expert', [(i, (i + turn) % length) for i in range(len...]
    dynamic_update_slice x0 -> x6, local copies, waits for them, and re-layouts: none -> 8.14 us  [body(): out = lax.dynamic_update_slice_in_dim(out, theirs, source, axis=0)]
    all_to_all x1 -> x0, starting transfers between devices: 3.7 us -> none  [body(): lax.all_to_all(outgoing, 'expert', split_axis=0, concat_axis=0, tiled=True)]
  transfers between devices with their start and end apart: 7 -> 12, of which waited for: 5 -> 7; matrix products, arithmetic and copies ran while one was open for 3% -> 6% of each run, Pallas kernels for 0% -> 0%
where the time goes in v1:
time: 342 us; the launch traced here: 341 us
  waiting for transfers between devices  166 us (49%)
  blocking collectives  82.5 us (24%)
  matrix products  30.8 us (9%)
  local copies, waits for them, and re-layouts  19.2 us (6%)
  starting transfers between devices  18.4 us (5%)
  between operations  13.3 us (4%)
  other arithmetic  11.4 us (3%)
    reduce_scatter x2, waiting for transfers between devices, body(): lax.psum_scatter(partial_value.astype(jnp.bfloat16), 'mp', scatter_dimens...  128 us
    all_gather x2, blocking collectives, rows_first(): whole, at, outs = (lax.all_gather(both, axis, axis=0, tiled=True), 0, [])  82.5 us
    ppermute x6, waiting for transfers between devices, body(): lax.ppermute(sent, 'expert', [(i, (i + turn) % length) for i in range(len...  25.4 us
    dot_general x2, matrix products, body(): jnp.dot(hidden, down_rows, preferred_element_type=jnp.float32)  18.8 us
    all_to_all x2, waiting for transfers between devices, body(): lax.all_to_all(summed.reshape(experts, tok_rows, slice_width), 'expert',...  11.9 us
    concatenate x2, other arithmetic, side_by_side(): both = jnp.concatenate(arrays, axis=along)  10.6 us
    ppermute x6, starting transfers between devices, body(): lax.ppermute(sent, 'expert', [(i, (i + turn) % length) for i in range(len...  9.6 us
    all_to_all x2, starting transfers between devices, body(): lax.all_to_all(summed.reshape(experts, tok_rows, slice_width), 'expert',...  8.46 us
  transfers between devices with their start and end apart: 12, of which 7 were waited for; matrix products, arithmetic and copies ran while one was open for 6% of the time, Pallas kernels for 0%

profile of v1, /device:TPU:40, one launch (start us, length us, event | category | flops | bytes accessed | tf_op | source)
XLA Modules:
  0.0 341.3 jit_solution(5185642565627566390)
XLA Ops:
  6.6 2.6 slice_bitcast_fusion.5
  9.2 0.5 copy-done.1
  9.7 1.1 copy-done.2
  10.8 2.7 slice_bitcast_fusion.3
  13.5 5.5 %pad_maximum_fusion = bf16[224,12288]{1,0:T(8,128)(2,1)} fusion(bf16[224,4096]{1,0:T(8,128)(2,1)S(1)} %get-tuple-element.11, bf16[224,4096]{1,0:T(8,128)(2,1)S(1)} %get-tuple-element.28, bf16[224,4096]{1,0:T(8,128)(2,1)S(1)} %get-tuple-element.7), kind=kLoop, calls=%fused_computation | loop fusion | flops 16515072 | bytes 11010048 | tf_op jit(solution)/shard_map/concatenate | solution.py:38
  19.2 0.5 copy-done.7
  19.8 0.1 copy.19
  20.1 51.8 %all_gather.12 = bf16[4096,65]{0,1:T(8,128)(2,1)S(1)} all-gather(bf16[256,65]{0,1:T(8,128)(2,1)S(1)} %pad_maximum_fusion.2), channel_id=1, replica_groups=mesh['groups'=2,'mp'=16,'expert'=4,'dp'=2] {'mp'}, dimensions={0}, use_global_device_ids=true | all-gather | bytes 565760 | tf_op jit(solution)/shard_map/all_gather | solution.py:25
  71.9 0.2 fusion.14
  72.1 0.9 convolution_convert_fusion.3
  73.0 1.3 copy-done
  74.3 0.1 dynamic-slice_bitcast_fusion.3
  74.4 1.7 collective-permute-start
  76.2 3.0 collective-permute-start.1
  79.2 1.3 collective-permute-start.2
  80.5 9.1 %collective-permute-done = bf16[1,1,64,4096]{3,2,0,1:T(8,128)(2,1)} collective-permute-done((bf16[1,1,64,4096]{3,2,0,1:T(8,128)(2,1)S(1)}, bf16[1,1,64,4096]{3,2,0,1:T(8,128)(2,1)}, u32[]{:S(2)}, u32[]{:S(2)}) %collective-permute-start) | collective-permute-done | bytes 524320 | tf_op jit(solution)/shard_map/ppermute | solution.py:82
  89.6 1.9 constant_dynamic-update-slice_fusion.5
  91.5 3.7 %collective-permute-done.1 = bf16[1,1,64,4096]{3,2,0,1:T(8,128)(2,1)} collective-permute-done((bf16[1,1,64,4096]{3,2,0,1:T(8,128)(2,1)S(1)}, bf16[1,1,64,4096]{3,2,0,1:T(8,128)(2,1)}, u32[]{:S(2)}, u32[]{:S(2)}) %collective-permute-start.1) | collective-permute-done | bytes 524320 | tf_op jit(solution)/shard_map/ppermute | solution.py:82
  95.2 1.9 constant_dynamic-update-slice_fusion.4
  97.1 1.9 constant_dynamic-update-slice_fusion.3
  99.0 3.8 %fusion.6 = f32[256,448]{0,1:T(8,128)S(1)} fusion(bf16[256,4096]{1,0:T(8,128)(2,1)} %bitcast.81, bf16[448,12288]{1,0:T(8,128)(2,1)} %all-gather.3.cloned.1.call-done), kind=kOutput, calls=%fused_computation.12 | convolution fusion | flops 939524096 | bytes 6225920 | tf_op jit(solution)/shard_map/dot_general | solution.py:90
  102.8 9.4 %convolution_convert_fusion.2 = bf16[256,4096]{1,0:T(8,128)(2,1)} fusion(bf16[448,12288]{1,0:T(8,128)(2,1)} %all-gather.3.cloned.1.call-done, f32[256,448]{0,1:T(8,128)S(1)} %fusion.6, bf16[256,4096]{1,0:T(8,128)(2,1)} %bitcast.82), kind=kOutput, calls=%fused_computation.4 | convolution fusion | flops 1880784896 | bytes 11993088 | tf_op jit(solution)/shard_map/dot_general | solution.py:92
  112.3 0.2 all-gather.5.cloned.1.call-start
  112.5 5.0 %pad_maximum_fusion.1 = bf16[224,12288]{1,0:T(8,128)(2,1)} fusion(bf16[224,4096]{1,0:T(8,128)(2,1)} %get-tuple-element.12, bf16[224,4096]{1,0:T(8,128)(2,1)} %get-tuple-element.27, bf16[224,4096]{1,0:T(8,128)(2,1)S(1)} %get-tuple-element.8), kind=kLoop, calls=%fused_computation.1 | loop fusion | flops 16515072 | bytes 11010048 | tf_op jit(solution)/shard_map/concatenate | solution.py:38
  117.7 0.1 copy.23
  117.8 0.1 reduce_window_sum.18
  117.9 0.3 copy-done.4
  118.3 58.2 %reduce-scatter.3.cloned.1.call-done = bf16[256,256]{1,0:T(8,128)(2,1)} async-done(((bf16[256,4096]{1,0:T(8,128)(2,1)}), bf16[256,256]{1,0:T(8,128)(2,1)}) %reduce-scatter.3.cloned.1.call-update) | async-done | bytes 131088 | tf_op jit(solution)/shard_map/reduce_scatter | solution.py:93
  176.5 4.3 %all-to-all-start = ((bf16[4,64,256]{2,1,0:T(8,128)(2,1)}), bf16[4,64,256]{2,1,0:T(8,128)(2,1)S(1)}, u32[]{:S(2)}, u32[]{:S(2)}) async-start(bf16[4,64,256]{2,1,0:T(8,128)(2,1)} %bitcast.83), calls=%async_computation.1 | async-start | bytes 262144 | tf_op jit(solution)/shard_map/all_to_all | solution.py:96
  180.8 6.0 %all-to-all-done = bf16[4,64,256]{2,1,0:T(8,128)(2,1)S(1)} async-done(((bf16[4,64,256]{2,1,0:T(8,128)(2,1)}), bf16[4,64,256]{2,1,0:T(8,128)(2,1)S(1)}, u32[]{:S(2)}, u32[]{:S(2)}) %all-to-all-start) | async-done | bytes 131104 | tf_op jit(solution)/shard_map/all_to_all | solution.py:96
  186.8 0.3 fusion.13
  187.1 30.7 %all_gather.14 = bf16[4096,65]{0,1:T(8,128)(2,1)S(1)} all-gather(bf16[256,65]{0,1:T(8,128)(2,1)S(1)} %pad_maximum_fusion.3), channel_id=1, replica_groups=mesh['groups'=2,'mp'=16,'expert'=4,'dp'=2] {'mp'}, dimensions={0}, use_global_device_ids=true | all-gather | bytes 565760 | tf_op jit(solution)/shard_map/all_gather | solution.py:25
  217.8 0.2 fusion.17
  218.0 2.2 convolution_convert_fusion.1
  220.2 1.5 dynamic-slice_bitcast_fusion
  221.7 0.7 collective-permute-start.3
  222.4 2.1 collective-permute-start.4
  224.4 0.8 collective-permute-start.5
  225.2 12.6 %collective-permute-done.3 = bf16[1,1,64,4096]{3,2,0,1:T(8,128)(2,1)S(1)} collective-permute-done((bf16[1,1,64,4096]{3,2,0,1:T(8,128)(2,1)S(1)}, bf16[1,1,64,4096]{3,2,0,1:T(8,128)(2,1)S(1)}, u32[]{:S(2)}, u32[]{:S(2)}) %collective-permute-start.3) | collective-permute-done | bytes 524320 | tf_op jit(solution)/shard_map/ppermute | solution.py:82
  237.8 0.8 constant_dynamic-update-slice_fusion.2
  238.6 0.8 constant_dynamic-update-slice_fusion.1
  239.5 0.8 constant_dynamic-update-slice_fusion
  240.3 3.9 %fusion.1 = f32[256,448]{0,1:T(8,128)S(1)} fusion(bf16[256,4096]{1,0:T(8,128)(2,1)} %bitcast.32, bf16[448,12288]{1,0:T(8,128)(2,1)} %all-gather.5.cloned.1.call-done), kind=kOutput, calls=%fused_computation.7 | convolution fusion | flops 939524096 | bytes 6225920 | tf_op jit(solution)/shard_map/dot_general | solution.py:90
  244.2 9.4 %convolution_convert_fusion = bf16[256,4096]{1,0:T(8,128)(2,1)} fusion(bf16[448,12288]{1,0:T(8,128)(2,1)} %all-gather.5.cloned.1.call-done, f32[256,448]{0,1:T(8,128)S(1)} %fusion.1, bf16[256,4096]{1,0:T(8,128)(2,1)} %bitcast.32), kind=kOutput, calls=%fused_computation.2 | convolution fusion | flops 1880784896 | bytes 11993088 | tf_op jit(solution)/shard_map/dot_general | solution.py:92
  253.6 70.0 %reduce-scatter.5.cloned.1.call-done = bf16[256,256]{1,0:T(8,128)(2,1)} async-done(((bf16[256,4096]{1,0:T(8,128)(2,1)}), bf16[256,256]{1,0:T(8,128)(2,1)}) %reduce-scatter.5.cloned.1.call-update) | async-done | bytes 131088 | tf_op jit(solution)/shard_map/reduce_scatter | solution.py:93
  323.6 4.2 %all-to-all-start.1 = ((bf16[4,64,256]{2,1,0:T(8,128)(2,1)}), bf16[4,64,256]{2,1,0:T(8,128)(2,1)S(1)}, u32[]{:S(2)}, u32[]{:S(2)}) async-start(bf16[4,64,256]{2,1,0:T(8,128)(2,1)} %bitcast.84), calls=%async_computation.3 | async-start | bytes 262144 | tf_op jit(solution)/shard_map/all_to_all | solution.py:96
  327.8 6.0 %all-to-all-done.1 = bf16[4,64,256]{2,1,0:T(8,128)(2,1)S(1)} async-done(((bf16[4,64,256]{2,1,0:T(8,128)(2,1)}), bf16[4,64,256]{2,1,0:T(8,128)(2,1)S(1)}, u32[]{:S(2)}, u32[]{:S(2)}) %all-to-all-start.1) | async-done | bytes 131104 | tf_op jit(solution)/shard_map/all_to_all | solution.py:96
  333.8 0.9 fusion.12
  (45 shorter events, 0.8 us)
Async XLA Ops:
  6.5 92.4 %all-gather.3.cloned.1.call-start = ((), (), s32[]{:S(2)}) async-start(), calls=%async_computation.4 | async-start | bytes 16515072 | tf_op jit(solution)/shard_map/all_gather | solution.py:39
  6.6 3.1 copy-start.1
  6.6 4.3 %copy-start.2 = (bf16[2,1,224,4096]{3,2,1,0:T(8,128)(2,1)S(1)}, bf16[2,1,224,4096]{3,2,1,0:T(8,128)(2,1)}, u32[]{:S(2)}) copy-start(bf16[2,1,224,4096]{3,2,1,0:T(8,128)(2,1)} %param.14) | copy-start | bytes 11010052
  19.0 0.7 copy-start.7
  19.0 0.7 copy-start.6
  19.1 1.0 copy-start.5
  19.1 1.0 copy-start.3
  19.1 157.4 %reduce-scatter.3.cloned.1.call-start = ((), (), s32[]{:S(2)}) async-start(), calls=%async_computation.5 | async-start | bytes 2228224 | tf_op jit(solution)/shard_map/reduce_scatter | solution.py:93
  73.0 1.3 copy-start
  74.4 15.2 %collective-permute-start = (bf16[1,1,64,4096]{3,2,0,1:T(8,128)(2,1)S(1)}, bf16[1,1,64,4096]{3,2,0,1:T(8,128)(2,1)}, u32[]{:S(2)}, u32[]{:S(2)}) collective-permute-start(bf16[1,1,64,4096]{3,2,0,1:T(8,128)(2,1)S(1)} %get-tuple-element.18), channel_id=1, source_target_pairs={{0,2},{2,4},{4,6},{6,0},{1,3},{3,5},{5,7},{7,1},{8,10},{10,12},{12... | collective-permute-start | bytes 1572872 | tf_op jit(solution)/shard_map/ppermute | solution.py:82
  76.2 19.1 %collective-permute-start.1 = (bf16[1,1,64,4096]{3,2,0,1:T(8,128)(2,1)S(1)}, bf16[1,1,64,4096]{3,2,0,1:T(8,128)(2,1)}, u32[]{:S(2)}, u32[]{:S(2)}) collective-permute-start(bf16[1,1,64,4096]{3,2,0,1:T(8,128)(2,1)S(1)} %get-tuple-element.17), channel_id=1, source_target_pairs={{0,4},{2,6},{4,0},{6,2},{1,5},{3,7},{5,1},{7,3},{8,12},{10,14},{12... | collective-permute-start | bytes 1572872 | tf_op jit(solution)/shard_map/ppermute | solution.py:82
  79.2 17.9 %collective-permute-start.2 = (bf16[1,1,64,4096]{3,2,0,1:T(8,128)(2,1)S(1)}, bf16[1,1,64,4096]{3,2,0,1:T(8,128)(2,1)}, u32[]{:S(2)}, u32[]{:S(2)}) collective-permute-start(bf16[1,1,64,4096]{3,2,0,1:T(8,128)(2,1)S(1)} %get-tuple-element.16), channel_id=1, source_target_pairs={{0,6},{2,0},{4,2},{6,4},{1,7},{3,1},{5,3},{7,5},{8,14},{10,8},{12,... | collective-permute-start | bytes 1572872 | tf_op jit(solution)/shard_map/ppermute | solution.py:82
  112.3 128.0 %all-gather.5.cloned.1.call-start = ((), (), s32[]{:S(2)}) async-start(), calls=%async_computation.6 | async-start | bytes 16515072 | tf_op jit(solution)/shard_map/all_gather | solution.py:39
  117.6 0.7 copy-start.4
  176.5 10.3 %all-to-all-start = ((bf16[4,64,256]{2,1,0:T(8,128)(2,1)}), bf16[4,64,256]{2,1,0:T(8,128)(2,1)S(1)}, u32[]{:S(2)}, u32[]{:S(2)}) async-start(bf16[4,64,256]{2,1,0:T(8,128)(2,1)} %bitcast.83), calls=%async_computation.1 | async-start | bytes 262144 | tf_op jit(solution)/shard_map/all_to_all | solution.py:96
  180.8 142.8 %reduce-scatter.5.cloned.1.call-start = ((), (), s32[]{:S(2)}) async-start(), calls=%async_computation.7 | async-start | bytes 2228224 | tf_op jit(solution)/shard_map/reduce_scatter | solution.py:93
  221.7 16.1 %collective-permute-start.3 = (bf16[1,1,64,4096]{3,2,0,1:T(8,128)(2,1)S(1)}, bf16[1,1,64,4096]{3,2,0,1:T(8,128)(2,1)S(1)}, u32[]{:S(2)}, u32[]{:S(2)}) collective-permute-start(bf16[1,1,64,4096]{3,2,0,1:T(8,128)(2,1)S(1)} %get-tuple-element.15), channel_id=1, source_target_pairs={{0,2},{2,4},{4,6},{6,0},{1,3},{3,5},{5,7},{7,1},{8,10},{10,12},{12... | collective-permute-start | bytes 1572872 | tf_op jit(solution)/shard_map/ppermute | solution.py:82
  222.4 16.3 %collective-permute-start.4 = (bf16[1,1,64,4096]{3,2,0,1:T(8,128)(2,1)S(1)}, bf16[1,1,64,4096]{3,2,0,1:T(8,128)(2,1)S(1)}, u32[]{:S(2)}, u32[]{:S(2)}) collective-permute-start(bf16[1,1,64,4096]{3,2,0,1:T(8,128)(2,1)S(1)} %get-tuple-element.14), channel_id=1, source_target_pairs={{0,4},{2,6},{4,0},{6,2},{1,5},{3,7},{5,1},{7,3},{8,12},{10,14},{12... | collective-permute-start | bytes 1572872 | tf_op jit(solution)/shard_map/ppermute | solution.py:82
  224.4 15.1 %collective-permute-start.5 = (bf16[1,1,64,4096]{3,2,0,1:T(8,128)(2,1)S(1)}, bf16[1,1,64,4096]{3,2,0,1:T(8,128)(2,1)S(1)}, u32[]{:S(2)}, u32[]{:S(2)}) collective-permute-start(bf16[1,1,64,4096]{3,2,0,1:T(8,128)(2,1)S(1)} %get-tuple-element.13), channel_id=1, source_target_pairs={{0,6},{2,0},{4,2},{6,4},{1,7},{3,1},{5,3},{7,5},{8,14},{10,8},{12,... | collective-permute-start | bytes 1572872 | tf_op jit(solution)/shard_map/ppermute | solution.py:82
  323.6 10.2 %all-to-all-start.1 = ((bf16[4,64,256]{2,1,0:T(8,128)(2,1)}), bf16[4,64,256]{2,1,0:T(8,128)(2,1)S(1)}, u32[]{:S(2)}, u32[]{:S(2)}) async-start(bf16[4,64,256]{2,1,0:T(8,128)(2,1)} %bitcast.84), calls=%async_computation.3 | async-start | bytes 262144 | tf_op jit(solution)/shard_map/all_to_all | solution.py:96
Sparse Core Ops, SparseCore 0:
  19.2 45.2 all-gather.2
  112.4 64.0 reduce-scatter.2
  178.4 29.6 all-gather.4
  253.7 69.8 reduce-scatter.4
